TPU v7x, 32 devices: a whole 2x2x4 slice. The times are simulated.
32 devices in a mesh: tile: 8 (over z, x), sub: 4 (over y, core).
Axes of the slice: x: 2, y: 2, z: 4, core: 2. Of those that a mesh axis runs over, the one named last changes fastest.
Arguments:
- initial_state: float32 [8, 64, 1024], P('tile', None, 'sub'), may hold values from -6 to 6
- cotangent: float32 [8, 64, 1024], P('tile', None, 'sub'), may hold values from -6 to 6
- w_in: bfloat16 [576, 1024], replicated, may hold values from -0.25 to 0.25
- b_in: float32 [1024], replicated, may hold values from -3 to 3
- w_out: bfloat16 [64, 1024], replicated, may hold values from -0.1875 to 0.1875
- edge_flips: int32 [8, 2], P('tile'), may hold values 0 or 1
Outputs:
- final_state: float32 [8, 64, 1024], P('tile', None, 'sub')
- grad_state: float32 [8, 64, 1024], P('tile', None, 'sub')
- grad_w_in: float32 [576, 1024], replicated
- grad_b_in: float32 [1024], replicated
- grad_w_out: float32 [64, 1024], replicated
All inputs are finite; a program needn't handle non-finite values. No bound on the sum of `edge_flips` on one device may be relied on, other than what follows from the above.
Results may differ from a plain program's by a relative error of at most 0.006.
Values may be sent and summed in bfloat16 or wider, within the bound.
A program may use at most 64 MiB of HBM per device.

v0:
```python
import functools

import jax
import jax.numpy as jnp
from jax import lax
from jax.experimental import pallas as pl
from jax.experimental.pallas import tpu as pltpu
from jax.sharding import PartitionSpec as P

STEPS = 4
TILE_ROW = 4
STEP_SIZE = 0.25
LEAD = 8
MESH = pl.DeviceIdType.MESH
F32 = jnp.float32
BF16 = jnp.bfloat16

LANES = 128


def layout(width, rows):
    names = [("NW", 1), ("NE", 1), ("SW", 1), ("SE", 1), ("N", width), ("S", width), ("W", rows), ("E", rows)]
    place, at = {}, 0
    for name, size in names:
        place[name] = (at, size)
        at += -(-size // 8) * 8
    return place, at


def reduce_plan(tiles, subs, flat_rows):
    bits = [("sub", 1 << i) for i in range(subs.bit_length() - 1)]
    bits += [("tile", 1 << i) for i in range(tiles.bit_length() - 1)]
    unit = 16 * tiles * subs
    units = -(-flat_rows // unit)
    count = min(3, units)
    groups, at = [], 0
    for g in range(count):
        size = (units // count + (1 if g < units % count else 0)) * unit
        turning = bits[1:4]
        order = bits[:1] + turning[g:] + turning[:g] + bits[4:]
        groups.append((at, size, order))
        at += size
    return groups, at


def dot(a, b, dims, precision=None):
    return lax.dot_general(a, b, (dims, ((), ())), preferred_element_type=F32, precision=precision)


def tree_sum(parts):
    while len(parts) > 1:
        parts = [parts[i] + parts[i + 1] if i + 1 < len(parts) else parts[i] for i in range(0, len(parts), 2)]
    return parts[0]


def chain_kernel(
    tiles, subs, rows, width, levels, hidden,
    state_hbm, cot_hbm, w_in_hbm, b_in_hbm, w_out_hbm, flips_hbm,
    final_ref, grad_ref, whole,
    state_ref, cot_ref, w_in_ref, b_in_ref, w_out_ref, flips_ref, load_sem,
    gw_in_ref, gb_ref, gw_out_ref,
    flat, out_half, in_half, red_ssem, red_rsem, gat_ssem, gat_rsem,
    send, recv, sum_out, sum_in,
    padded, pad_grad, edge, field, gradient, totals, center, w_sum, hid, slope, patch,
    gp32, gp16, shifts,
    halo_ssem, halo_rsem, sum_ssem, sum_rsem,
):
    place, _ = layout(width, rows)
    cols = rows * width
    count = tiles * subs
    inv_total = 1.0 / (count * cols)
    me_t, me_s = lax.axis_index("tile"), lax.axis_index("sub")
    me = me_t * subs + me_s
    first, last = me_s == 0, me_s == subs - 1
    wide = width + 2 * LEAD
    in_width = w_in_ref.shape[0]
    unroll = count <= 64

    loads = [
        pltpu.make_async_copy(src, dst, load_sem.at[i])
        for i, (src, dst) in enumerate((
            (state_hbm, state_ref), (cot_hbm, cot_ref), (flips_hbm, flips_ref),
            (w_out_hbm, w_out_ref), (b_in_hbm, b_in_ref), (w_in_hbm, w_in_ref)))
    ]
    for load in loads:
        load.start()

    def device_at(by):
        other = lax.rem(me + by, count)
        return (other // subs, lax.rem(other, subs))

    barrier = pltpu.get_barrier_semaphore()

    def greet(by, carry):
        pl.semaphore_signal(barrier, inc=1, device_id=device_at(by), device_id_type=MESH)
        return carry

    lax.fori_loop(1, count, greet, 0, unroll=unroll)

    def tile_at(by):
        return lax.rem(me_t + by + 2 * tiles, tiles)

    def north_of(by):
        return (jnp.where(first, tile_at(by - TILE_ROW), tile_at(by)), jnp.where(first, subs - 1, me_s - 1))

    def south_of(by):
        return (jnp.where(last, tile_at(by + TILE_ROW), tile_at(by)), jnp.where(last, 0, me_s + 1))

    targets = {
        "N": north_of(0), "S": south_of(0), "W": (tile_at(-1), me_s), "E": (tile_at(1), me_s),
        "NW": north_of(-1), "NE": north_of(1), "SW": south_of(-1), "SE": south_of(1),
    }

    def halo_copies(p):
        out = []
        for i, (name, (at, size)) in enumerate(place.items()):
            out.append(pltpu.make_async_remote_copy(
                src_ref=send.at[p, pl.ds(at, size)], dst_ref=recv.at[p, pl.ds(at, size)],
                send_sem=halo_ssem.at[p, i], recv_sem=halo_rsem.at[p, i],
                device_id=targets[name], device_id_type=MESH))
        return out

    def start_halos(p):
        for copy in halo_copies(p):
            copy.start()

    def wait_halos(p):
        for copy in halo_copies(p):
            copy.wait()

    def start_sums(p, a, b):
        sum_out[p, 0:1] = jnp.concatenate([a, b], axis=1)

        def begin(by, carry):
            pltpu.make_async_remote_copy(
                src_ref=sum_out.at[p, pl.ds(0, 1)], dst_ref=sum_in.at[p, by - 1, pl.ds(0, 1)],
                send_sem=sum_ssem.at[p], recv_sem=sum_rsem.at[p],
                device_id=device_at(by), device_id_type=MESH).start()
            return carry

        lax.fori_loop(1, count, begin, 0, unroll=unroll)

    def wait_sums(p):
        pltpu.make_async_remote_copy(
            src_ref=sum_in.at[p, :, pl.ds(0, 1)], dst_ref=sum_in.at[p, :, pl.ds(0, 1)],
            send_sem=sum_ssem.at[p], recv_sem=sum_rsem.at[p],
            device_id=device_at(1), device_id_type=MESH).wait()
        if count <= 64:
            total = tree_sum([sum_out[p, 0:1]] + [sum_in[p, d, 0:1] for d in range(count - 1)])
        else:
            total = sum_out[p, 0:1] + jnp.sum(sum_in[p, :, 0:1], axis=0)
        return total[:, :levels], total[:, levels:]

    at_row = lax.broadcasted_iota(jnp.int32, (wide, wide), 0)
    at_col = lax.broadcasted_iota(jnp.int32, (wide, wide), 1)
    same = (at_row == at_col).astype(F32)
    turned = (at_row + at_col == wide - 1).astype(F32)
    diagonal = (
        lax.broadcasted_iota(jnp.int32, (levels, levels), 0) == lax.broadcasted_iota(jnp.int32, (levels, levels), 1)
    ).astype(F32)

    def column(line):
        return jnp.sum(diagonal * line, axis=1, keepdims=True)

    def seam_matrix(flag, here):
        mix = jnp.where(here, flag, 0).astype(F32)
        return turned * mix + same * (1.0 - mix)

    def send_field(p):
        for name, row in (("N", 0), ("S", rows - 1)):
            at = place[name][0]
            line = field[row * width:(row + 1) * width]
            send[p, at:at + width] = line
            for side, cell in (("W", 0), ("E", width - 1)):
                corner = place[name + side][0]
                send[p, corner:corner + 1] = line[cell:cell + 1]
        for name, cell in (("W", 0), ("E", width - 1)):
            at = place[name][0]
            for r in range(rows):
                send[p, at + r:at + r + 1] = field[r * width + cell:r * width + cell + 1]

    def pad_field(p, shift):
        for name, cell in (("E", LEAD - 1), ("W", LEAD + width)):
            at = place[name][0]
            for r in range(rows):
                padded[r + 1, cell:cell + 1] = recv[p, at + r:at + r + 1] - shift
        for name, row, flag in (("S", 0, 0), ("N", rows + 1, 1)):
            at = place[name][0]
            edge[LEAD:LEAD + width] = recv[p, at:at + width] - shift
            for side, cell in (("E", LEAD - 1), ("W", LEAD + width)):
                corner = place[name + side][0]
                edge[cell:cell + 1] = recv[p, corner:corner + 1] - shift
            padded[row] = dot(turns[flag].astype(BF16), edge[...].astype(BF16), ((1,), (0,)))

    edge[...] = jnp.zeros_like(edge)
    padded[...] = jnp.zeros_like(padded)
    center[...] = jnp.zeros_like(center)
    totals[...] = jnp.zeros_like(totals)
    nothing = jnp.zeros((1, levels), F32)
    loads[0].wait()
    field[...] = state_ref[0].T
    send_field(0)
    loads[1].wait()
    gradient[...] = cot_ref[0].T
    cot_sum = jnp.sum(gradient[...], axis=0, keepdims=True)
    pl.semaphore_wait(barrier, count - 1)
    start_halos(0)
    start_sums(0, nothing, cot_sum)
    loads[2].wait()
    turns = [
        seam_matrix(flips_ref[0:1, 0:1], first),
        seam_matrix(flips_ref[0:1, 1:2], last),
    ]
    gw_in_ref[...] = jnp.zeros_like(gw_in_ref)
    gb_ref[...] = jnp.zeros_like(gb_ref)
    gw_out_ref[...] = jnp.zeros_like(gw_out_ref)
    for load in loads[3:]:
        load.wait()
    w_sum[...] = w_in_ref[0:levels].astype(F32)
    for o in range(1, 9):
        w_sum[...] += w_in_ref[o * levels:(o + 1) * levels].astype(F32)

    def forward(k, carry):
        mid = center[0:1]
        padded[1:rows + 1, LEAD:LEAD + width, :] = (field[...] - mid).reshape(rows, width, levels)
        wait_halos(k)
        pad_field(k, mid)
        for a in range(3):
            for b in range(3):
                o = 3 * a + b
                piece = padded[a:a + rows, LEAD - 1 + b:LEAD - 1 + b + width, :]
                patch[k, :, o * levels:(o + 1) * levels] = piece.reshape(cols, levels).astype(BF16)
        act = dot(patch[k], w_in_ref[...], ((1,), (0,)))
        sum_a, sum_b = wait_sums(k)
        shift = sum_a * (STEP_SIZE * inv_total)
        totals[1:2] += sum_b
        move = mid - shift
        shifts[k, 0:1] = move
        act = act + (b_in_ref[...] + jnp.sum(w_sum[...] * column(move), axis=0, keepdims=True))
        sig = jax.nn.sigmoid(act)
        low = (act * sig).astype(BF16)
        hid[k] = low
        tendency = dot(low, w_out_ref[...], ((1,), (1,)))
        field[...] = (field[...] - shift) + STEP_SIZE * tendency
        own = jnp.sum(tendency, axis=0, keepdims=True)

        @pl.when(k < STEPS - 1)
        def _():
            send_field(k + 1)
            start_halos(k + 1)
            start_sums(k + 1, own, nothing)

        center[0:1] = own * (STEP_SIZE / cols)
        center[1:2] = own
        slope[k] = sig * (1.0 + act * (1.0 - sig))
        return carry

    lax.fori_loop(0, STEPS, forward, 0)

    def gradient_through(k, j):
        mid = jnp.sum(gradient[...], axis=0, keepdims=True) * (STEP_SIZE / cols)
        gh = dot((STEP_SIZE * gradient[...] - mid).astype(BF16), w_out_ref[...], ((1,), (0,)))

        @pl.when(j > 0)
        def _():
            sum_a, sum_b = wait_sums(STEPS + j - 1)
            totals[0:1] += sum_a
            totals[1:2] += sum_b

        level_grad = totals[1:2] * (STEP_SIZE * inv_total)
        lift = jnp.sum(w_out_ref[...].astype(F32) * column(mid - level_grad), axis=0, keepdims=True)
        gp = (gh + lift) * slope[k]
        gp32[...] = gp
        gp16[...] = gp.astype(BF16)
        return level_grad

    def spread(p, sums):
        gi = dot(gp16[...], w_in_ref[...], ((1,), (1,)))
        pad_grad[...] = jnp.zeros_like(pad_grad)
        if sums is not None:
            gi_sum = jnp.sum(gi, axis=0, keepdims=True)
            part = tree_sum([gi_sum[:, o * levels:(o + 1) * levels] for o in range(9)])
            start_sums(p, sums, part)
        for a in range(3):
            for b in range(3):
                o = 3 * a + b
                piece = gi[:, o * levels:(o + 1) * levels].reshape(rows, width, levels)
                pad_grad[a:a + rows, LEAD - 1 + b:LEAD - 1 + b + width, :] += piece
        for name, row, flag in (("N", 0, 0), ("S", rows + 1, 1)):
            at = place[name][0]
            edge[...] = dot(turns[flag], pad_grad[row], ((1,), (0,)), lax.Precision.HIGHEST)
            send[p, at:at + width] = edge[LEAD:LEAD + width]
            for side, cell in (("W", LEAD - 1), ("E", LEAD + width)):
                corner = place[name + side][0]
                send[p, corner:corner + 1] = edge[cell:cell + 1]
        for name, cell in (("W", LEAD - 1), ("E", LEAD + width)):
            at = place[name][0]
            for r in range(rows):
                send[p, at + r:at + r + 1] = pad_grad[r + 1, cell:cell + 1]
        start_halos(p)

    def weigh(k, level_grad):
        gp_sum = jnp.sum(gp32[...], axis=0, keepdims=True)
        gb_ref[...] += gp_sum
        back = column(shifts[k, 0:1]) * gp_sum
        gw = dot(patch[k], gp16[...], ((0,), (0,)))
        for o in range(9):
            part = slice(o * levels, (o + 1) * levels)
            gw_in_ref[part] += gw[part] + back
        low_gt = (STEP_SIZE * gradient[...] - level_grad).astype(BF16)
        gw_out_ref[...] += dot(low_gt, hid[k], ((0,), (0,)))

    def collect(p):
        for name, row in (("N", rows - 1), ("S", 0)):
            at = place[name][0]
            gradient[row * width:(row + 1) * width] += recv[p, at:at + width]
            for side, cell in (("W", width - 1), ("E", 0)):
                corner = place[name + side][0]
                gradient[row * width + cell:row * width + cell + 1] += recv[p, corner:corner + 1]
        for name, cell in (("W", width - 1), ("E", 0)):
            at = place[name][0]
            for r in range(rows):
                gradient[r * width + cell:r * width + cell + 1] += recv[p, at + r:at + r + 1]

    def backward(j, carry):
        k = STEPS - 1 - j
        p = STEPS + j
        level_grad = gradient_through(k, j)
        spread(p, jnp.where(j == 0, center[1:2], 0.0))
        weigh(k, level_grad)
        gradient[...] += pad_grad[1:rows + 1, LEAD:LEAD + width, :].reshape(cols, levels)
        wait_halos(p)
        collect(p)
        return carry

    lax.fori_loop(0, STEPS - 1, backward, 0)
    level_grad = gradient_through(0, STEPS - 1)
    weigh(0, level_grad)

    stride = in_width + levels + 8
    groups, flat_rows = reduce_plan(tiles, subs, stride * (hidden // LANES))
    for c in range(hidden // LANES):
        at, lanes = c * stride, slice(c * LANES, (c + 1) * LANES)
        flat[at:at + in_width] = gw_in_ref[:, lanes]
        flat[at + in_width:at + in_width + levels] = gw_out_ref[:, lanes]
        flat[at + in_width + levels:at + stride] = jnp.broadcast_to(gb_ref[:, lanes], (8, LANES))
    used = stride * (hidden // LANES)
    if flat_rows > used:
        flat[used:flat_rows] = jnp.zeros((flat_rows - used, LANES), F32)

    def bit_of(axis, step):
        index = me_t if axis == "tile" else me_s
        return lax.rem(index // step, 2)

    def peer_of(axis, step):
        if axis == "tile":
            return (me_t + step * (1 - 2 * bit_of(axis, step)), me_s)
        return (me_t, me_s + step * (1 - 2 * bit_of(axis, step)))

    def bases(group):
        start, size, order = group
        out, base = [], start
        for axis, step in order:
            out.append((base, size // 2))
            size = size // 2
            base = base + bit_of(axis, step) * size
        return out, base, size

    depth = len(groups[0][2])

    def reduce_copy(g, i):
        start, size, order = groups[g]
        half = size >> (i + 1)
        at = start + size - (size >> i)
        return pltpu.make_async_remote_copy(
            src_ref=out_half.at[pl.ds(at, half)], dst_ref=in_half.at[pl.ds(at, half)],
            send_sem=red_ssem.at[g, i], recv_sem=red_rsem.at[g, i],
            device_id=peer_of(*order[i]), device_id_type=MESH)

    def gather_copy(g, i):
        start, size, order = groups[g]
        part = size >> (i + 1)
        base = bases(groups[g])[0][i][0] + bit_of(*order[i]) * part
        rows_here = pl.ds(pl.multiple_of(base, 16), part)
        return pltpu.make_async_remote_copy(
            src_ref=whole.at[rows_here], dst_ref=whole.at[rows_here],
            send_sem=gat_ssem.at[g, i], recv_sem=gat_rsem.at[g, i],
            device_id=peer_of(*order[i]), device_id_type=MESH)

    for i in range(depth + 1):
        for g, (start, size, order) in enumerate(groups):
            levels_of = bases((start, size, order))
            if i > 0:
                reduce_copy(g, i - 1).wait()
                base, half = levels_of[0][i - 1]
                at = start + size - (size >> (i - 1))
                kept = pl.ds(pl.multiple_of(base + bit_of(*order[i - 1]) * half, 16), half)
                flat[kept] = flat[kept] + in_half[at:at + half].astype(F32)
            if i < depth:
                base, half = levels_of[0][i]
                at = start + size - (size >> i)
                away = pl.ds(pl.multiple_of(base + (1 - bit_of(*order[i])) * half, 16), half)
                out_half[at:at + half] = flat[away].astype(BF16)
                reduce_copy(g, i).start()
            else:
                own = pl.ds(pl.multiple_of(levels_of[1], 16), levels_of[2])
                whole[own] = flat[own].astype(BF16)
                gather_copy(g, depth - 1).start()
        if i == 1:
            spread(2 * STEPS - 1, None)
            gradient[...] += pad_grad[1:rows + 1, LEAD:LEAD + width, :].reshape(cols, levels)
            final_ref[0] = (field[...] - totals[0:1] * (STEP_SIZE * inv_total)).T
        if i == depth - 1:
            wait_halos(2 * STEPS - 1)
            collect(2 * STEPS - 1)
            grad_ref[0] = gradient[...].T
    for i in reversed(range(depth)):
        for g in range(len(groups)):
            gather_copy(g, i).wait()
            if i > 0:
                gather_copy(g, i - 1).start()


def finish_kernel(hidden, final_in, grad_in, whole, final_ref, grad_ref, gw_in_ref, gb_ref, gw_out_ref, wide_in, wide_b, wide_out, sem):
    in_width, levels = gw_in_ref.shape[0], gw_out_ref.shape[0]
    stride = in_width + levels + 8
    copies = [
        pltpu.make_async_copy(final_in, final_ref, sem.at[0]),
        pltpu.make_async_copy(grad_in, grad_ref, sem.at[1]),
    ]
    for copy in copies:
        copy.start()
    chunks = hidden // LANES
    for c in range(chunks):
        at, lanes = c * stride, slice(c * LANES, (c + 1) * LANES)
        wide_in[c] = whole[at:at + in_width].astype(F32)
        copies.append(pltpu.make_async_copy(wide_in.at[c], gw_in_ref.at[:, pl.ds(c * LANES, LANES)], sem.at[4 + c]))
        copies[-1].start()
        wide_out[:, lanes] = whole[at + in_width:at + in_width + levels].astype(F32)
        tail = whole[at + in_width + levels - 8:at + stride].astype(F32)
        wide_b[:, lanes] = tail[8:9]
    copies.append(pltpu.make_async_copy(wide_out, gw_out_ref, sem.at[2]))
    copies[-1].start()
    copies.append(pltpu.make_async_copy(wide_b, gb_ref, sem.at[3]))
    copies[-1].start()
    for copy in copies:
        copy.wait()


def shards(tiles, subs, initial_state, cotangent, w_in, b_in, w_out, edge_flips):
    _, levels, cols = initial_state.shape
    in_width, hidden = w_in.shape
    side = 1
    while side * side < cols * subs:
        side += 1
    rows, width = side // subs, side
    _, buffer_rows = layout(width, rows)
    phases = 2 * STEPS
    count = tiles * subs
    groups, flat_rows = reduce_plan(tiles, subs, (in_width + levels + 8) * (hidden // LANES))
    depth = len(groups[0][2])
    wide = width + 2 * LEAD
    vmem = pl.BlockSpec(memory_space=pltpu.VMEM)
    hbm = pl.BlockSpec(memory_space=pltpu.HBM)
    final, grad, whole = pl.pallas_call(
        functools.partial(chain_kernel, tiles, subs, rows, width, levels, hidden),
        out_shape=(
            jax.ShapeDtypeStruct(initial_state.shape, F32),
            jax.ShapeDtypeStruct(initial_state.shape, F32),
            jax.ShapeDtypeStruct((flat_rows, LANES), BF16),
        ),
        in_specs=[hbm] * 6,
        out_specs=[vmem] * 3,
        scratch_shapes=[
            pltpu.VMEM(initial_state.shape, F32),
            pltpu.VMEM(initial_state.shape, F32),
            pltpu.VMEM((in_width, hidden), BF16),
            pltpu.VMEM((1, hidden), F32),
            pltpu.VMEM((levels, hidden), BF16),
            pltpu.VMEM(edge_flips.shape, jnp.int32),
            pltpu.SemaphoreType.DMA((6,)),
            pltpu.VMEM((in_width, hidden), F32),
            pltpu.VMEM((1, hidden), F32),
            pltpu.VMEM((levels, hidden), F32),
            pltpu.VMEM((flat_rows, LANES), F32),
            pltpu.VMEM((flat_rows, LANES), BF16),
            pltpu.VMEM((flat_rows, LANES), BF16),
            pltpu.SemaphoreType.DMA((len(groups), depth)),
            pltpu.SemaphoreType.DMA((len(groups), depth)),
            pltpu.SemaphoreType.DMA((len(groups), depth)),
            pltpu.SemaphoreType.DMA((len(groups), depth)),
            pltpu.VMEM((phases, buffer_rows, levels), F32),
            pltpu.VMEM((phases, buffer_rows, levels), F32),
            pltpu.VMEM((phases, 8, 2 * levels), F32),
            pltpu.VMEM((phases, count - 1, 8, 2 * levels), F32),
            pltpu.VMEM((rows + 2, wide, levels), F32),
            pltpu.VMEM((rows + 2, wide, levels), F32),
            pltpu.VMEM((wide, levels), F32),
            pltpu.VMEM((cols, levels), F32),
            pltpu.VMEM((cols, levels), F32),
            pltpu.VMEM((8, levels), F32),
            pltpu.VMEM((8, levels), F32),
            pltpu.VMEM((levels, hidden), F32),
            pltpu.VMEM((STEPS, cols, hidden), BF16),
            pltpu.VMEM((STEPS, cols, hidden), F32),
            pltpu.VMEM((STEPS, cols, in_width), BF16),
            pltpu.VMEM((cols, hidden), F32),
            pltpu.VMEM((cols, hidden), BF16),
            pltpu.VMEM((STEPS, 8, levels), F32),
            pltpu.SemaphoreType.DMA((phases, 8)),
            pltpu.SemaphoreType.DMA((phases, 8)),
            pltpu.SemaphoreType.DMA((phases,)),
            pltpu.SemaphoreType.DMA((phases,)),
        ],
        compiler_params=pltpu.CompilerParams(has_side_effects=True, collective_id=0, vmem_limit_bytes=44 * 1024 * 1024),
        name="chain",
    )(*[pltpu.with_memory_space_constraint(v, pltpu.HBM) for v in (initial_state, cotangent, w_in, b_in[None, :], w_out, edge_flips)])
    final, grad, gw_in, gb, gw_out = pl.pallas_call(
        functools.partial(finish_kernel, hidden),
        out_shape=(
            jax.ShapeDtypeStruct(initial_state.shape, F32),
            jax.ShapeDtypeStruct(initial_state.shape, F32),
            jax.ShapeDtypeStruct((in_width, hidden), F32),
            jax.ShapeDtypeStruct((1, hidden), F32),
            jax.ShapeDtypeStruct((levels, hidden), F32),
        ),
        in_specs=[vmem] * 3,
        out_specs=[hbm] * 5,
        scratch_shapes=[
            pltpu.VMEM((hidden // LANES, in_width, LANES), F32),
            pltpu.VMEM((1, hidden), F32),
            pltpu.VMEM((levels, hidden), F32),
            pltpu.SemaphoreType.DMA((4 + hidden // LANES,)),
        ],
        compiler_params=pltpu.CompilerParams(vmem_limit_bytes=8 * 1024 * 1024),
        name="finish",
    )(final, grad, whole)
    return (final, grad, gw_in, gb[0], gw_out)


def solution(mesh):
    in_specs = (P("tile", None, "sub"), P("tile", None, "sub"), P(), P(), P(), P("tile", None))
    out_specs = (P("tile", None, "sub"), P("tile", None, "sub"), P(), P(), P())
    body = functools.partial(shards, mesh.shape["tile"], mesh.shape["sub"])
    return jax.shard_map(body, mesh=mesh, in_specs=in_specs, out_specs=out_specs, check_vma=False)
```

profile of v0, /device:TPU:0, one launch (start us, length us, event | category | flops | bytes accessed | tf_op | source)
XLA Modules:
  0.0 82.3 jit_solution(17909662972615830082)
XLA Ops:
  0.6 80.0 %chain.1 = (f32[1,64,256]{2,1,0:T(8,128)S(1)}, f32[1,64,256]{2,1,0:T(8,128)S(1)}, bf16[5632,128]{1,0:T(8,128)(2,1)S(1)}) custom-call(f32[1,64,256]{2,1,0:T(8,128)} %state_hbm.1, f32[1,64,256]{2,1,0:T(8,128)} %cot_hbm.1, bf16[576,1024]{1,0:T(8,128)(2,1)} %w_in_hbm.1, f32[1,1024]{1,0:T(1,128)} %bitcast.2, bf16[64,1024]{1,0:T(8,128)(2,1)} %w_out_hbm.1, ...), custom_call_target="tpu_custom_call" | custom-call | tf_op jit(solution)/shard_map/chain/pallas_call | solution.py:465
  80.6 1.6 %finish.1 = (f32[1,64,256]{2,1,0:T(8,128)}, f32[1,64,256]{2,1,0:T(8,128)}, f32[576,1024]{1,0:T(8,128)}, f32[1,1024]{1,0:T(1,128)}, f32[64,1024]{1,0:T(8,128)}) custom-call(f32[1,64,256]{2,1,0:T(8,128)S(1)} %get-tuple-element.13.final_in, f32[1,64,256]{2,1,0:T(8,128)S(1)} %get-tuple-element.14.grad_in, bf16[5632,128]{1,0:T(8,128)(2,1)S(1)} %get-tuple-element.15.whole), custom_call_target="tpu_custom_call" | custom-call | tf_op jit(solution)/shard_map/finish/pallas_call | solution.py:518
where the time goes:
time: 82.4 us; the launch traced here: 82.3 us
  Pallas kernels  81.6 us (99%)
    pallas_call x1, Pallas kernels, shards(): pl.pallas_call(functools.partial(chain_kernel, tiles, subs, rows, width,...  80 us

commit v1 on v0

v1 whole, which is shorter than its diff:
```python
import functools

import jax
import jax.numpy as jnp
from jax import lax
from jax.experimental import pallas as pl
from jax.experimental.pallas import tpu as pltpu
from jax.sharding import PartitionSpec as P

STEPS = 4
TILE_ROW = 4
STEP_SIZE = 0.25
LEAD = 8
MESH = pl.DeviceIdType.MESH
F32 = jnp.float32
BF16 = jnp.bfloat16

LANES = 128


def layout(width, rows):
    names = [("NW", 1), ("NE", 1), ("SW", 1), ("SE", 1), ("N", width), ("S", width), ("W", rows), ("E", rows)]
    place, at = {}, 0
    for name, size in names:
        place[name] = (at, size)
        at += -(-size // 8) * 8
    return place, at


def reduce_plan(tiles, subs, flat_rows):
    sub_bits = [("sub", 1 << i) for i in range(subs.bit_length() - 1)]
    tile_bits = [("tile", 1 << i) for i in range(tiles.bit_length() - 1)]
    rest = sub_bits[1:] + tile_bits
    pairs = [tuple(rest[i:i + 2]) for i in range(0, len(rest), 2)]
    orders = [[tuple(sub_bits[:1])] + pairs, [tuple(sub_bits[:1])] + pairs[1:2] + pairs[:1] + pairs[2:]]
    unit = 8 * tiles * subs
    units = -(-flat_rows // unit)
    shares = [0, 0, 0, 0]
    for n, part in enumerate((0.3, 0.5, 0.8, 1.0)):
        shares[n] = int(round(units * part)) - sum(shares[:n])
    groups, at = [], 0
    for n, share in enumerate(shares):
        if share:
            groups.append((at, share * unit, orders[n % 2]))
            at += share * unit
    return groups, at


def dot(a, b, dims, precision=None):
    return lax.dot_general(a, b, (dims, ((), ())), preferred_element_type=F32, precision=precision)


def tree_sum(parts):
    while len(parts) > 1:
        parts = [parts[i] + parts[i + 1] if i + 1 < len(parts) else parts[i] for i in range(0, len(parts), 2)]
    return parts[0]


def chain_kernel(
    tiles, subs, rows, width, levels, hidden,
    state_hbm, cot_hbm, w_in_hbm, b_in_hbm, w_out_hbm, flips_hbm,
    final_ref, grad_ref, whole, gb_ref,
    state_ref, cot_ref, w_in_ref, b_in_ref, w_out_ref, flips_ref, load_sem,
    flat, out_half, in_half, red_ssem, red_rsem, gat_ssem, gat_rsem,
    gb_sum, gb_out, gb_in, gb_far, gb_ssem, gb_rsem,
    send, recv, sum_out, sum_in,
    padded, pad_grad, edge, lines, ends, field, gradient, totals, center, w_sum, hid, slope, patch, patch_t,
    rim, pre, gp_sum, gp16, shifts,
    halo_ssem, halo_rsem, sum_ssem, sum_rsem,
):
    place, _ = layout(width, rows)
    cols = rows * width
    count = tiles * subs
    inv_total = 1.0 / (count * cols)
    me_t, me_s = lax.axis_index("tile"), lax.axis_index("sub")
    me = me_t * subs + me_s
    first, last = me_s == 0, me_s == subs - 1
    wide = width + 2 * LEAD
    in_width = w_in_ref.shape[0]
    stride = in_width + levels
    chunks = hidden // LANES
    groups, flat_rows = reduce_plan(tiles, subs, stride * chunks)
    rim_rows = -(-rows // 16) * 16
    unroll = count <= 64

    loads = [
        pltpu.make_async_copy(src, dst, load_sem.at[i])
        for i, (src, dst) in enumerate((
            (state_hbm, state_ref), (cot_hbm, cot_ref), (flips_hbm, flips_ref),
            (w_out_hbm, w_out_ref), (b_in_hbm, b_in_ref), (w_in_hbm, w_in_ref)))
    ]
    for load in loads:
        load.start()

    def device_at(by):
        other = lax.rem(me + by, count)
        return (other // subs, lax.rem(other, subs))

    barrier = pltpu.get_barrier_semaphore()

    def greet(by, carry):
        pl.semaphore_signal(barrier, inc=1, device_id=device_at(by), device_id_type=MESH)
        return carry

    lax.fori_loop(1, count, greet, 0, unroll=unroll)

    def tile_at(by):
        return lax.rem(me_t + by + 2 * tiles, tiles)

    def north_of(by):
        return (jnp.where(first, tile_at(by - TILE_ROW), tile_at(by)), jnp.where(first, subs - 1, me_s - 1))

    def south_of(by):
        return (jnp.where(last, tile_at(by + TILE_ROW), tile_at(by)), jnp.where(last, 0, me_s + 1))

    targets = {
        "N": north_of(0), "S": south_of(0), "W": (tile_at(-1), me_s), "E": (tile_at(1), me_s),
        "NW": north_of(-1), "NE": north_of(1), "SW": south_of(-1), "SE": south_of(1),
    }

    def halo_copies(p):
        out = []
        for i, (name, (at, size)) in enumerate(place.items()):
            out.append(pltpu.make_async_remote_copy(
                src_ref=send.at[p, pl.ds(at, size)], dst_ref=recv.at[p, pl.ds(at, size)],
                send_sem=halo_ssem.at[p, i], recv_sem=halo_rsem.at[p, i],
                device_id=targets[name], device_id_type=MESH))
        return out

    def start_halos(p):
        for copy in halo_copies(p):
            copy.start()

    def wait_halos(p):
        for copy in halo_copies(p):
            copy.wait()

    def start_sums(p, a, b):
        sum_out[p, 0:1] = jnp.concatenate([a, b], axis=1)

        def begin(by, carry):
            pltpu.make_async_remote_copy(
                src_ref=sum_out.at[p, pl.ds(0, 1)], dst_ref=sum_in.at[p, by - 1, pl.ds(0, 1)],
                send_sem=sum_ssem.at[p], recv_sem=sum_rsem.at[p],
                device_id=device_at(by), device_id_type=MESH).start()
            return carry

        lax.fori_loop(1, count, begin, 0, unroll=unroll)

    def wait_sums(p):
        pltpu.make_async_remote_copy(
            src_ref=sum_in.at[p, :, pl.ds(0, 1)], dst_ref=sum_in.at[p, :, pl.ds(0, 1)],
            send_sem=sum_ssem.at[p], recv_sem=sum_rsem.at[p],
            device_id=device_at(1), device_id_type=MESH).wait()
        if count <= 64:
            total = tree_sum([sum_out[p, 0:1]] + [sum_in[p, d, 0:1] for d in range(count - 1)])
        else:
            total = sum_out[p, 0:1] + jnp.sum(sum_in[p, :, 0:1], axis=0)
        return total[:, :levels], total[:, levels:]

    at_row = lax.broadcasted_iota(jnp.int32, (wide, wide), 0)
    at_col = lax.broadcasted_iota(jnp.int32, (wide, wide), 1)
    same = (at_row == at_col).astype(F32)
    turned = (at_row + at_col == wide - 1).astype(F32)
    diagonal = (
        lax.broadcasted_iota(jnp.int32, (levels, levels), 0) == lax.broadcasted_iota(jnp.int32, (levels, levels), 1)
    ).astype(F32)

    def column(flat_line):
        return jnp.sum(diagonal * flat_line, axis=1, keepdims=True)

    def turn_exact(turn, value):
        high = value.astype(BF16)
        left = value - high.astype(F32)
        middle = left.astype(BF16)
        low = (left - middle.astype(F32)).astype(BF16)
        parts = dot(turn.astype(BF16), jnp.concatenate([high, middle, low], axis=1), ((1,), (0,)))
        return parts[:, :levels] + parts[:, levels:2 * levels] + parts[:, 2 * levels:]

    def seam_matrix(flag, here):
        mix = jnp.where(here, flag, 0).astype(F32)
        return turned * mix + same * (1.0 - mix)

    def send_field(p):
        for name, row in (("N", 0), ("S", rows - 1)):
            at = place[name][0]
            line = field[row * width:(row + 1) * width]
            send[p, at:at + width] = line
            for side, cell in (("W", 0), ("E", width - 1)):
                corner = place[name + side][0]
                send[p, corner:corner + 1] = line[cell:cell + 1]
        for name, cell in (("W", 0), ("E", width - 1)):
            at = place[name][0]
            for r in range(rows):
                send[p, at + r:at + r + 1] = field[r * width + cell:r * width + cell + 1]

    def gather_patch():
        for a in range(3):
            for b in range(3):
                o = 3 * a + b
                piece = padded[a:a + rows, LEAD - 1 + b:LEAD - 1 + b + width, :]
                patch[:, o * levels:(o + 1) * levels] = piece.reshape(cols, levels).astype(BF16)

    def gather_rim(p, shift):
        for n, name in enumerate(("S", "N")):
            at = place[name][0]
            edge[LEAD:LEAD + width] = recv[p, at:at + width] - shift
            for side, cell in (("E", LEAD - 1), ("W", LEAD + width)):
                corner = place[name + side][0]
                edge[cell:cell + 1] = recv[p, corner:corner + 1] - shift
            lines[n] = dot(turns[n].astype(BF16), edge[...].astype(BF16), ((1,), (0,)))
            for b in range(3):
                o = 6 * n + b
                rim[n * width:(n + 1) * width, o * levels:(o + 1) * levels] = (
                    lines[n, LEAD - 1 + b:LEAD - 1 + b + width].astype(BF16))
        for n, name in enumerate(("E", "W")):
            at = place[name][0]
            ends[n, LEAD:LEAD + rows] = recv[p, at:at + rows] - shift
            at = 2 * width + n * rim_rows
            for a in range(3):
                o = 3 * a + 2 * n
                rim[at:at + rows, o * levels:(o + 1) * levels] = (
                    ends[n, LEAD - 1 + a:LEAD - 1 + a + rows].astype(BF16))

    def add_rim():
        extra = dot(rim[...], w_in_ref[...], ((1,), (0,)))
        pre[0:width] += extra[0:width]
        pre[cols - width:cols] += extra[width:2 * width]
        for n, cell in ((0, 0), (1, width - 1)):
            for r in range(rows):
                at, row = r * width + cell, 2 * width + n * rim_rows + r
                pre[at:at + 1] += extra[row:row + 1]

    def whole_patch(k):
        for n, row in ((0, 0), (1, rows + 1)):
            padded[row] = lines[n]
        for n, cell in ((0, LEAD - 1), (1, LEAD + width)):
            for r in range(rows):
                padded[r + 1, cell:cell + 1] = ends[n, LEAD + r:LEAD + r + 1]
        gather_patch()
        patch_t[k] = patch[...].T
        for row in (0, rows + 1):
            padded[row] = jnp.zeros((wide, levels), F32)
        for cell in (LEAD - 1, LEAD + width):
            padded[1:rows + 1, cell:cell + 1] = jnp.zeros((rows, 1, levels), F32)

    edge[...] = jnp.zeros_like(edge)
    padded[...] = jnp.zeros_like(padded)
    center[...] = jnp.zeros_like(center)
    totals[...] = jnp.zeros_like(totals)
    nothing = jnp.zeros((1, levels), F32)
    loads[0].wait()
    field[...] = state_ref[0].T
    send_field(0)
    loads[1].wait()
    gradient[...] = cot_ref[0].T
    cot_sum = jnp.sum(gradient[...], axis=0, keepdims=True)
    pl.semaphore_wait(barrier, count - 1)
    start_halos(0)
    start_sums(0, nothing, cot_sum)
    loads[2].wait()
    turns = [
        seam_matrix(flips_ref[0:1, 0:1], first),
        seam_matrix(flips_ref[0:1, 1:2], last),
    ]
    flat[...] = jnp.zeros_like(flat)
    gb_sum[...] = jnp.zeros_like(gb_sum)
    ends[...] = jnp.zeros_like(ends)
    rim[...] = jnp.zeros_like(rim)
    for load in loads[3:]:
        load.wait()
    w_sum[...] = w_in_ref[0:levels].astype(F32)
    for o in range(1, 9):
        w_sum[...] += w_in_ref[o * levels:(o + 1) * levels].astype(F32)

    def forward(k, carry):
        mid = center[0:1]
        padded[1:rows + 1, LEAD:LEAD + width, :] = (field[...] - mid).reshape(rows, width, levels)
        gather_patch()
        pre[...] = dot(patch[...], w_in_ref[...], ((1,), (0,)))
        wait_halos(k)
        gather_rim(k, mid)
        add_rim()
        sum_a, sum_b = wait_sums(k)
        shift = sum_a * (STEP_SIZE * inv_total)
        totals[1:2] += sum_b
        move = mid - shift
        shifts[k, 0:1] = move
        act = pre[...] + (b_in_ref[...] + jnp.sum(w_sum[...] * column(move), axis=0, keepdims=True))
        sig = jax.nn.sigmoid(act)
        low = (act * sig).astype(BF16)
        hid[k] = low
        tendency = dot(low, w_out_ref[...], ((1,), (1,)))
        field[...] = (field[...] - shift) + STEP_SIZE * tendency
        own = jnp.sum(tendency, axis=0, keepdims=True)

        @pl.when(k < STEPS - 1)
        def _():
            send_field(k + 1)
            start_halos(k + 1)
            start_sums(k + 1, own, nothing)

        center[0:1] = own * (STEP_SIZE / cols)
        center[1:2] = own
        slope[k] = sig * (1.0 + act * (1.0 - sig))
        whole_patch(k)
        return carry

    lax.fori_loop(0, STEPS, forward, 0)

    def gradient_through(k, j):
        mid = jnp.sum(gradient[...], axis=0, keepdims=True) * (STEP_SIZE / cols)
        gh = dot((STEP_SIZE * gradient[...] - mid).astype(BF16), w_out_ref[...], ((1,), (0,)))

        @pl.when(j > 0)
        def _():
            sum_a, sum_b = wait_sums(STEPS + j - 1)
            totals[0:1] += sum_a
            totals[1:2] += sum_b

        level_grad = totals[1:2] * (STEP_SIZE * inv_total)
        lift = jnp.sum(w_out_ref[...].astype(F32) * column(mid - level_grad), axis=0, keepdims=True)
        gp = (gh + lift) * slope[k]
        gp16[...] = gp.astype(BF16)
        gp_sum[0:1] = jnp.sum(gp, axis=0, keepdims=True)
        return level_grad

    def spread(p, sums):
        gi = dot(gp16[...], w_in_ref[...], ((1,), (1,)))
        pad_grad[...] = jnp.zeros_like(pad_grad)
        if sums is not None:
            gi_sum = jnp.sum(gi, axis=0, keepdims=True)
            start_sums(p, sums, tree_sum([gi_sum[:, o * levels:(o + 1) * levels] for o in range(9)]))
        for a in range(3):
            for b in range(3):
                o = 3 * a + b
                piece = gi[:, o * levels:(o + 1) * levels].reshape(rows, width, levels)
                pad_grad[a:a + rows, LEAD - 1 + b:LEAD - 1 + b + width, :] += piece
        for n, (name, row) in enumerate((("N", 0), ("S", rows + 1))):
            at = place[name][0]
            edge[...] = turn_exact(turns[n], pad_grad[row])
            send[p, at:at + width] = edge[LEAD:LEAD + width]
            for side, cell in (("W", LEAD - 1), ("E", LEAD + width)):
                corner = place[name + side][0]
                send[p, corner:corner + 1] = edge[cell:cell + 1]
        for name, cell in (("W", LEAD - 1), ("E", LEAD + width)):
            at = place[name][0]
            for r in range(rows):
                send[p, at + r:at + r + 1] = pad_grad[r + 1, cell:cell + 1]
        start_halos(p)

    def keep():
        gradient[...] += pad_grad[1:rows + 1, LEAD:LEAD + width, :].reshape(cols, levels)

    def weigh(k, low_gt, c, many):
        lanes = slice(c * LANES, (c + many) * LANES)
        back = column(shifts[k, 0:1]) * gp_sum[0:1, lanes]
        gw = dot(patch_t[k], gp16[:, lanes], ((1,), (0,)))
        gw_out = dot(low_gt, hid[k, :, lanes], ((1,), (0,)))
        for n in range(many):
            at, part = (c + n) * stride, slice(n * LANES, (n + 1) * LANES)
            for o in range(9):
                flat[at + o * levels:at + (o + 1) * levels] += gw[o * levels:(o + 1) * levels, part] + back[:, part]
            flat[at + in_width:at + stride] += gw_out[:, part]

    def gradient_low(level_grad):
        return (STEP_SIZE * gradient[...] - level_grad).T.astype(BF16)

    def collect(p):
        for name, row in (("N", rows - 1), ("S", 0)):
            at = place[name][0]
            gradient[row * width:(row + 1) * width] += recv[p, at:at + width]
            for side, cell in (("W", width - 1), ("E", 0)):
                corner = place[name + side][0]
                gradient[row * width + cell:row * width + cell + 1] += recv[p, corner:corner + 1]
        for name, cell in (("W", width - 1), ("E", 0)):
            at = place[name][0]
            for r in range(rows):
                gradient[r * width + cell:r * width + cell + 1] += recv[p, at + r:at + r + 1]

    def backward(j, carry):
        k = STEPS - 1 - j
        p = STEPS + j
        level_grad = gradient_through(k, j)
        spread(p, jnp.where(j == 0, center[1:2], 0.0))
        low_gt = gradient_low(level_grad)
        keep()
        gb_sum[...] += gp_sum[0:1]
        weigh(k, low_gt, 0, chunks)
        wait_halos(p)
        collect(p)
        return carry

    lax.fori_loop(0, STEPS - 1, backward, 0)
    level_grad = gradient_through(0, STEPS - 1)
    low_gt = gradient_low(level_grad)

    def bit_of(bit):
        axis, step = bit
        return lax.rem((me_t if axis == "tile" else me_s) // step, 2)

    def peer_of(bits, mask):
        at = {"tile": me_t, "sub": me_s}
        for i, (axis, step) in enumerate(bits):
            if mask >> i & 1:
                at[axis] = at[axis] + step * (1 - 2 * bit_of((axis, step)))
        return (at["tile"], at["sub"])

    def place_of(bits, mask):
        index = 0
        for i, bit in enumerate(bits):
            index = index + (1 - bit_of(bit) if mask >> i & 1 else bit_of(bit)) * (1 << i)
        return index

    stages = []
    for start, size, order in groups:
        base, at, found = start, start, []
        for bits in order:
            piece = size >> len(bits)
            found.append((base, piece, at, bits))
            at += size - piece
            base = base + place_of(bits, 0) * piece
            size = piece
        stages.append((found, base, size))

    def rows_at(base, piece):
        return pl.ds(pl.multiple_of(base, 8), piece)

    def reduce_copies(g, i):
        base, piece, at, bits = stages[g][0][i]
        return [pltpu.make_async_remote_copy(
            src_ref=out_half.at[pl.ds(at + (m - 1) * piece, piece)],
            dst_ref=in_half.at[pl.ds(at + (m - 1) * piece, piece)],
            send_sem=red_ssem.at[g, i, m - 1], recv_sem=red_rsem.at[g, i, m - 1],
            device_id=peer_of(bits, m), device_id_type=MESH) for m in range(1, 1 << len(bits))]

    def reduce_start(g, i):
        base, piece, at, bits = stages[g][0][i]
        for m, copy in enumerate(reduce_copies(g, i), 1):
            away = flat[rows_at(base + place_of(bits, m) * piece, piece)]
            out_half[at + (m - 1) * piece:at + m * piece] = away.astype(BF16)
            copy.start()

    def reduce_wait(g, i):
        base, piece, at, bits = stages[g][0][i]
        own = rows_at(base + place_of(bits, 0) * piece, piece)
        total = flat[own]
        for m, copy in enumerate(reduce_copies(g, i), 1):
            copy.wait()
            total = total + in_half[at + (m - 1) * piece:at + m * piece].astype(F32)
        flat[own] = total

    def gather_copies(g, i):
        base, piece, at, bits = stages[g][0][i]
        own = rows_at(base + place_of(bits, 0) * piece, piece)
        return [pltpu.make_async_remote_copy(
            src_ref=whole.at[own], dst_ref=whole.at[own],
            send_sem=gat_ssem.at[g, i, m - 1], recv_sem=gat_rsem.at[g, i, m - 1],
            device_id=peer_of(bits, m), device_id_type=MESH) for m in range(1, 1 << len(bits))]

    near = tuple([("sub", 1 << i) for i in range(subs.bit_length() - 1)] + [("tile", 1)])
    far = tuple(("tile", 1 << i) for i in range(1, tiles.bit_length() - 1))

    def bias_copies(n):
        bits, source, slots = ((near, gb_out, gb_in), (far, gb_ref, gb_far))[n]
        return [pltpu.make_async_remote_copy(
            src_ref=source, dst_ref=slots.at[place_of(bits, 0)], send_sem=gb_ssem.at[n, m - 1], recv_sem=gb_rsem.at[n, m - 1],
            device_id=peer_of(bits, m), device_id_type=MESH) for m in range(1, 1 << len(bits))]

    def bias_start(n):
        bits, source, slots = ((near, gb_out, gb_in), (far, gb_ref, gb_far))[n]
        slots[place_of(bits, 0)] = source[...]
        for copy in bias_copies(n):
            copy.start()

    def bias_wait(n):
        for copy in bias_copies(n):
            copy.wait()
        slots = (gb_in, gb_far)[n]
        gb_ref[...] = tree_sum([slots[d] for d in range(slots.shape[0])])

    for c in range(chunks):
        lanes = slice(c * LANES, (c + 1) * LANES)
        gb_out[c:c + 1] = gb_sum[0:1, lanes] + gp_sum[0:1, lanes]
    bias_start(0)
    started = 0
    for c in range(0, chunks, 2):
        weigh(0, low_gt, c, 2)
        while started < len(groups) and (c + 2 == chunks or groups[started][0] + groups[started][1] <= (c + 2) * stride):
            reduce_start(started, 0)
            started += 1
    depth = max(len(order) for _, _, order in groups)
    for i in range(1, depth + 1):
        for g in range(len(groups)):
            reduce_wait(g, i - 1)
            if i < depth:
                reduce_start(g, i)
            else:
                _, base, size = stages[g]
                own = rows_at(base, size)
                whole[own] = flat[own].astype(BF16)
                for copy in gather_copies(g, depth - 1):
                    copy.start()
        if i == 1:
            spread(2 * STEPS - 1, None)
            keep()
            final_ref[0] = (field[...] - totals[0:1] * (STEP_SIZE * inv_total)).T
            bias_wait(0)
            bias_start(1)
        if i == 2:
            wait_halos(2 * STEPS - 1)
            collect(2 * STEPS - 1)
            grad_ref[0] = gradient[...].T
            bias_wait(1)
    for i in reversed(range(depth)):
        for g in range(len(groups)):
            for copy in gather_copies(g, i):
                copy.wait()
            if i > 0:
                for copy in gather_copies(g, i - 1):
                    copy.start()


def finish_kernel(hidden, final_in, grad_in, whole, gb_in, final_ref, grad_ref, gw_in_ref, gb_ref, gw_out_ref, wide_in, wide_out, sem):
    in_width, levels = gw_in_ref.shape[0], gw_out_ref.shape[0]
    stride = in_width + levels
    copies = [
        pltpu.make_async_copy(final_in, final_ref, sem.at[0]),
        pltpu.make_async_copy(grad_in, grad_ref, sem.at[1]),
        pltpu.make_async_copy(gb_in, gb_ref, sem.at[3]),
    ]
    for copy in copies:
        copy.start()
    for c in range(hidden // LANES):
        at, lanes = c * stride, slice(c * LANES, (c + 1) * LANES)
        wide_in[c] = whole[at:at + in_width].astype(F32)
        copies.append(pltpu.make_async_copy(wide_in.at[c], gw_in_ref.at[:, pl.ds(c * LANES, LANES)], sem.at[4 + c]))
        copies[-1].start()
        wide_out[:, lanes] = whole[at + in_width:at + stride].astype(F32)
    copies.append(pltpu.make_async_copy(wide_out, gw_out_ref, sem.at[2]))
    copies[-1].start()
    for copy in copies:
        copy.wait()


def shards(tiles, subs, initial_state, cotangent, w_in, b_in, w_out, edge_flips):
    _, levels, cols = initial_state.shape
    in_width, hidden = w_in.shape
    side = 1
    while side * side < cols * subs:
        side += 1
    rows, width = side // subs, side
    _, buffer_rows = layout(width, rows)
    phases = 2 * STEPS
    count = tiles * subs
    groups, flat_rows = reduce_plan(tiles, subs, (in_width + levels) * (hidden // LANES))
    depth = len(groups[0][2])
    chunks = hidden // LANES
    rim_rows = -(-rows // 16) * 16
    most = max(2 * subs, tiles // 2)
    wide = width + 2 * LEAD
    vmem = pl.BlockSpec(memory_space=pltpu.VMEM)
    hbm = pl.BlockSpec(memory_space=pltpu.HBM)
    final, grad, whole, gb = pl.pallas_call(
        functools.partial(chain_kernel, tiles, subs, rows, width, levels, hidden),
        out_shape=(
            jax.ShapeDtypeStruct(initial_state.shape, F32),
            jax.ShapeDtypeStruct(initial_state.shape, F32),
            jax.ShapeDtypeStruct((flat_rows, LANES), BF16),
            jax.ShapeDtypeStruct((chunks, LANES), F32),
        ),
        in_specs=[hbm] * 6,
        out_specs=[vmem] * 4,
        scratch_shapes=[
            pltpu.VMEM(initial_state.shape, F32),
            pltpu.VMEM(initial_state.shape, F32),
            pltpu.VMEM((in_width, hidden), BF16),
            pltpu.VMEM((1, hidden), F32),
            pltpu.VMEM((levels, hidden), BF16),
            pltpu.VMEM(edge_flips.shape, jnp.int32),
            pltpu.SemaphoreType.DMA((6,)),
            pltpu.VMEM((flat_rows, LANES), F32),
            pltpu.VMEM((flat_rows, LANES), BF16),
            pltpu.VMEM((flat_rows, LANES), BF16),
            pltpu.SemaphoreType.DMA((len(groups), depth, 3)),
            pltpu.SemaphoreType.DMA((len(groups), depth, 3)),
            pltpu.SemaphoreType.DMA((len(groups), depth, 3)),
            pltpu.SemaphoreType.DMA((len(groups), depth, 3)),
            pltpu.VMEM((1, hidden), F32),
            pltpu.VMEM((chunks, LANES), F32),
            pltpu.VMEM((2 * subs, chunks, LANES), F32),
            pltpu.VMEM((tiles // 2, chunks, LANES), F32),
            pltpu.SemaphoreType.DMA((2, most)),
            pltpu.SemaphoreType.DMA((2, most)),
            pltpu.VMEM((phases, buffer_rows, levels), F32),
            pltpu.VMEM((phases, buffer_rows, levels), F32),
            pltpu.VMEM((phases, 8, 2 * levels), F32),
            pltpu.VMEM((phases, count - 1, 8, 2 * levels), F32),
            pltpu.VMEM((rows + 2, wide, levels), F32),
            pltpu.VMEM((rows + 2, wide, levels), F32),
            pltpu.VMEM((wide, levels), F32),
            pltpu.VMEM((2, wide, levels), F32),
            pltpu.VMEM((2, rows + 2 * LEAD, levels), F32),
            pltpu.VMEM((cols, levels), F32),
            pltpu.VMEM((cols, levels), F32),
            pltpu.VMEM((8, levels), F32),
            pltpu.VMEM((8, levels), F32),
            pltpu.VMEM((levels, hidden), F32),
            pltpu.VMEM((STEPS, cols, hidden), BF16),
            pltpu.VMEM((STEPS, cols, hidden), F32),
            pltpu.VMEM((cols, in_width), BF16),
            pltpu.VMEM((STEPS, in_width, cols), BF16),
            pltpu.VMEM((2 * width + 2 * rim_rows, in_width), BF16),
            pltpu.VMEM((cols, hidden), F32),
            pltpu.VMEM((8, hidden), F32),
            pltpu.VMEM((cols, hidden), BF16),
            pltpu.VMEM((STEPS, 8, levels), F32),
            pltpu.SemaphoreType.DMA((phases, 8)),
            pltpu.SemaphoreType.DMA((phases, 8)),
            pltpu.SemaphoreType.DMA((phases,)),
            pltpu.SemaphoreType.DMA((phases,)),
        ],
        compiler_params=pltpu.CompilerParams(has_side_effects=True, collective_id=0, vmem_limit_bytes=44 * 1024 * 1024),
        name="chain",
    )(*[pltpu.with_memory_space_constraint(v, pltpu.HBM) for v in (initial_state, cotangent, w_in, b_in[None, :], w_out, edge_flips)])
    final, grad, gw_in, gb, gw_out = pl.pallas_call(
        functools.partial(finish_kernel, hidden),
        out_shape=(
            jax.ShapeDtypeStruct(initial_state.shape, F32),
            jax.ShapeDtypeStruct(initial_state.shape, F32),
            jax.ShapeDtypeStruct((in_width, hidden), F32),
            jax.ShapeDtypeStruct((chunks, LANES), F32),
            jax.ShapeDtypeStruct((levels, hidden), F32),
        ),
        in_specs=[vmem] * 4,
        out_specs=[hbm] * 5,
        scratch_shapes=[
            pltpu.VMEM((hidden // LANES, in_width, LANES), F32),
            pltpu.VMEM((levels, hidden), F32),
            pltpu.SemaphoreType.DMA((4 + hidden // LANES,)),
        ],
        compiler_params=pltpu.CompilerParams(vmem_limit_bytes=8 * 1024 * 1024),
        name="finish",
    )(final, grad, whole, gb)
    return (final, grad, gw_in, gb.reshape(hidden), gw_out)


def solution(mesh):
    in_specs = (P("tile", None, "sub"), P("tile", None, "sub"), P(), P(), P(), P("tile", None))
    out_specs = (P("tile", None, "sub"), P("tile", None, "sub"), P(), P(), P())
    body = functools.partial(shards, mesh.shape["tile"], mesh.shape["sub"])
    return jax.shard_map(body, mesh=mesh, in_specs=in_specs, out_specs=out_specs, check_vma=False)
```

time: 82.4 us -> 73.7 us (0.89)
  Pallas kernels: 81.6 us -> 72.9 us
    pallas_call x1, Pallas kernels: 80 us -> 71.3 us  [shards(): pl.pallas_call(functools.partial(chain_kernel, tiles, subs, rows, width,...]
where the time goes in v1:
time: 73.7 us; the launch traced here: 73.5 us
  Pallas kernels  72.9 us (99%)
    pallas_call x1, Pallas kernels, shards(): pl.pallas_call(functools.partial(chain_kernel, tiles, subs, rows, width,...  71.3 us
    pallas_call x1, Pallas kernels, shards(): pl.pallas_call(functools.partial(finish_kernel, hidden), out_shape=(jax.S...  1.63 us

profile of v1, /device:TPU:0, one launch (start us, length us, event | category | flops | bytes accessed | tf_op | source)
XLA Modules:
  0.0 73.5 jit_solution(16046839255068679828)
XLA Ops:
  0.6 71.3 %chain.1 = (f32[1,64,256]{2,1,0:T(8,128)S(1)}, f32[1,64,256]{2,1,0:T(8,128)S(1)}, bf16[5120,128]{1,0:T(8,128)(2,1)S(1)}, f32[8,128]{1,0:T(8,128)S(1)}) custom-call(f32[1,64,256]{2,1,0:T(8,128)} %state_hbm.1, f32[1,64,256]{2,1,0:T(8,128)} %cot_hbm.1, bf16[576,1024]{1,0:T(8,128)(2,1)} %w_in_hbm.1, f32[1,1024]{1,0:T(1,128)} %bitcast.2, ...), custom_call_target="tpu_custom_call" | custom-call | tf_op jit(solution)/shard_map/chain/pallas_call | solution.py:564
  71.9 1.6 %finish.1 = (f32[1,64,256]{2,1,0:T(8,128)}, f32[1,64,256]{2,1,0:T(8,128)}, f32[576,1024]{1,0:T(8,128)}, f32[8,128]{1,0:T(8,128)}, f32[64,1024]{1,0:T(8,128)}) custom-call(f32[1,64,256]{2,1,0:T(8,128)S(1)} %get-tuple-element.14.final_in, f32[1,64,256]{2,1,0:T(8,128)S(1)} %get-tuple-element.15.grad_in, bf16[5120,128]{1,0:T(8,128)(2,1)S(1)} %get-tuple-element.16.whole, ...), custom_call_target="tpu_custom_call" | custom-call | tf_op jit(solution)/shard_map/finish/pallas_call | solution.py:626

commit v2 on v1

--- a/solution.py
+++ b/solution.py
@@ -65,7 +65,7 @@
     gb_sum, gb_out, gb_in, gb_far, gb_ssem, gb_rsem,
     send, recv, sum_out, sum_in,
     padded, pad_grad, edge, lines, ends, field, gradient, totals, center, w_sum, hid, slope, patch, patch_t,
-    rim, pre, gp_sum, gp16, shifts,
+    rim, sides, w_side, pre, gp_sum, gp16, shifts,
     halo_ssem, halo_rsem, sum_ssem, sum_rsem,
 ):
     place, _ = layout(width, rows)
@@ -80,7 +80,6 @@
     stride = in_width + levels
     chunks = hidden // LANES
     groups, flat_rows = reduce_plan(tiles, subs, stride * chunks)
-    rim_rows = -(-rows // 16) * 16
     unroll = count <= 64
 
     loads = [
@@ -131,9 +130,10 @@
         for copy in halo_copies(p):
             copy.start()
 
-    def wait_halos(p):
-        for copy in halo_copies(p):
-            copy.wait()
+    def wait_halos(p, some=tuple(place)):
+        for name, copy in zip(place, halo_copies(p)):
+            if name in some:
+                copy.wait()
 
     def start_sums(p, a, b):
         sum_out[p, 0:1] = jnp.concatenate([a, b], axis=1)
@@ -177,8 +177,7 @@
         parts = dot(turn.astype(BF16), jnp.concatenate([high, middle, low], axis=1), ((1,), (0,)))
         return parts[:, :levels] + parts[:, levels:2 * levels] + parts[:, 2 * levels:]
 
-    def seam_matrix(flag, here):
-        mix = jnp.where(here, flag, 0).astype(F32)
+    def seam_matrix(mix):
         return turned * mix + same * (1.0 - mix)
 
     def send_field(p):
@@ -201,42 +200,43 @@
                 piece = padded[a:a + rows, LEAD - 1 + b:LEAD - 1 + b + width, :]
                 patch[:, o * levels:(o + 1) * levels] = piece.reshape(cols, levels).astype(BF16)
 
-    def gather_rim(p, shift):
+    def add_lines(p, shift):
         for n, name in enumerate(("S", "N")):
             at = place[name][0]
             edge[LEAD:LEAD + width] = recv[p, at:at + width] - shift
-            for side, cell in (("E", LEAD - 1), ("W", LEAD + width)):
-                corner = place[name + side][0]
-                edge[cell:cell + 1] = recv[p, corner:corner + 1] - shift
             lines[n] = dot(turns[n].astype(BF16), edge[...].astype(BF16), ((1,), (0,)))
             for b in range(3):
-                o = 6 * n + b
-                rim[n * width:(n + 1) * width, o * levels:(o + 1) * levels] = (
+                rim[n * width:(n + 1) * width, b * levels:(b + 1) * levels] = (
                     lines[n, LEAD - 1 + b:LEAD - 1 + b + width].astype(BF16))
+            extra = dot(rim[n * width:(n + 1) * width], w_in_ref[6 * n * levels:(6 * n + 3) * levels], ((1,), (0,)))
+            at = n * (cols - width)
+            pre[at:at + width] += extra
+
+    def add_sides(p, shift):
+        def corner(name):
+            at = place[name][0]
+            return recv[p, at:at + 1] - shift
+
         for n, name in enumerate(("E", "W")):
             at = place[name][0]
+            other = "WE"[n]
             ends[n, LEAD:LEAD + rows] = recv[p, at:at + rows] - shift
-            at = 2 * width + n * rim_rows
+            ends[n, LEAD - 1:LEAD] = jnp.where(mixes[0] > 0.5, corner("S" + other), corner("S" + name))
+            ends[n, LEAD + rows:LEAD + rows + 1] = jnp.where(mixes[1] > 0.5, corner("N" + other), corner("N" + name))
             for a in range(3):
-                o = 3 * a + 2 * n
-                rim[at:at + rows, o * levels:(o + 1) * levels] = (
+                sides[n, 0:rows, a * levels:(a + 1) * levels] = (
                     ends[n, LEAD - 1 + a:LEAD - 1 + a + rows].astype(BF16))
-
-    def add_rim():
-        extra = dot(rim[...], w_in_ref[...], ((1,), (0,)))
-        pre[0:width] += extra[0:width]
-        pre[cols - width:cols] += extra[width:2 * width]
-        for n, cell in ((0, 0), (1, width - 1)):
+            extra = dot(sides[n], w_side[n], ((1,), (0,)))
             for r in range(rows):
-                at, row = r * width + cell, 2 * width + n * rim_rows + r
-                pre[at:at + 1] += extra[row:row + 1]
+                at = r * width + n * (width - 1)
+                pre[at:at + 1] += extra[r:r + 1]
 
     def whole_patch(k):
         for n, row in ((0, 0), (1, rows + 1)):
             padded[row] = lines[n]
         for n, cell in ((0, LEAD - 1), (1, LEAD + width)):
-            for r in range(rows):
-                padded[r + 1, cell:cell + 1] = ends[n, LEAD + r:LEAD + r + 1]
+            for r in range(rows + 2):
+                padded[r, cell:cell + 1] = ends[n, LEAD - 1 + r:LEAD + r]
         gather_patch()
         patch_t[k] = patch[...].T
         for row in (0, rows + 1):
@@ -244,31 +244,35 @@
         for cell in (LEAD - 1, LEAD + width):
             padded[1:rows + 1, cell:cell + 1] = jnp.zeros((rows, 1, levels), F32)
 
+    nothing = jnp.zeros((1, levels), F32)
+    loads[0].wait()
+    field[...] = state_ref[0].T
+    send_field(0)
+    pl.semaphore_wait(barrier, count - 1)
+    start_halos(0)
+    loads[1].wait()
+    gradient[...] = cot_ref[0].T
+    start_sums(0, nothing, jnp.sum(gradient[...], axis=0, keepdims=True))
     edge[...] = jnp.zeros_like(edge)
     padded[...] = jnp.zeros_like(padded)
     center[...] = jnp.zeros_like(center)
     totals[...] = jnp.zeros_like(totals)
-    nothing = jnp.zeros((1, levels), F32)
-    loads[0].wait()
-    field[...] = state_ref[0].T
-    send_field(0)
-    loads[1].wait()
-    gradient[...] = cot_ref[0].T
-    cot_sum = jnp.sum(gradient[...], axis=0, keepdims=True)
-    pl.semaphore_wait(barrier, count - 1)
-    start_halos(0)
-    start_sums(0, nothing, cot_sum)
     loads[2].wait()
-    turns = [
-        seam_matrix(flips_ref[0:1, 0:1], first),
-        seam_matrix(flips_ref[0:1, 1:2], last),
+    mixes = [
+        jnp.where(first, flips_ref[0:1, 0:1], 0).astype(F32),
+        jnp.where(last, flips_ref[0:1, 1:2], 0).astype(F32),
     ]
+    turns = [seam_matrix(mix) for mix in mixes]
     flat[...] = jnp.zeros_like(flat)
     gb_sum[...] = jnp.zeros_like(gb_sum)
     ends[...] = jnp.zeros_like(ends)
-    rim[...] = jnp.zeros_like(rim)
+    sides[...] = jnp.zeros_like(sides)
     for load in loads[3:]:
         load.wait()
+    for n in range(2):
+        for a in range(3):
+            o = 3 * a + 2 * n
+            w_side[n, a * levels:(a + 1) * levels] = w_in_ref[o * levels:(o + 1) * levels]
     w_sum[...] = w_in_ref[0:levels].astype(F32)
     for o in range(1, 9):
         w_sum[...] += w_in_ref[o * levels:(o + 1) * levels].astype(F32)
@@ -278,17 +282,19 @@
         padded[1:rows + 1, LEAD:LEAD + width, :] = (field[...] - mid).reshape(rows, width, levels)
         gather_patch()
         pre[...] = dot(patch[...], w_in_ref[...], ((1,), (0,)))
-        wait_halos(k)
-        gather_rim(k, mid)
-        add_rim()
+        wait_halos(k, ("N", "S"))
+        add_lines(k, mid)
+        wait_halos(k, ("W", "E", "NW", "NE", "SW", "SE"))
+        add_sides(k, mid)
         sum_a, sum_b = wait_sums(k)
         shift = sum_a * (STEP_SIZE * inv_total)
         totals[1:2] += sum_b
         move = mid - shift
         shifts[k, 0:1] = move
-        act = pre[...] + (b_in_ref[...] + jnp.sum(w_sum[...] * column(move), axis=0, keepdims=True))
-        sig = jax.nn.sigmoid(act)
-        low = (act * sig).astype(BF16)
+        lift = b_in_ref[...] + jnp.sum(w_sum[...] * column(move), axis=0, keepdims=True)
+        gp_sum[1:2] = lift
+        act = pre[...] + lift
+        low = (act * jax.nn.sigmoid(act)).astype(BF16)
         hid[k] = low
         tendency = dot(low, w_out_ref[...], ((1,), (1,)))
         field[...] = (field[...] - shift) + STEP_SIZE * tendency
@@ -302,7 +308,9 @@
 
         center[0:1] = own * (STEP_SIZE / cols)
         center[1:2] = own
-        slope[k] = sig * (1.0 + act * (1.0 - sig))
+        value = pre[...] + gp_sum[1:2]
+        sig = jax.nn.sigmoid(value)
+        slope[k] = sig * (1.0 + value * (1.0 - sig))
         whole_patch(k)
         return carry
 
@@ -352,15 +360,16 @@
     def keep():
         gradient[...] += pad_grad[1:rows + 1, LEAD:LEAD + width, :].reshape(cols, levels)
 
-    def weigh(k, low_gt, c, many):
+    def weigh(k, low_gt, c, many, shifted=True):
         lanes = slice(c * LANES, (c + many) * LANES)
-        back = column(shifts[k, 0:1]) * gp_sum[0:1, lanes]
+        back = column(shifts[k, 0:1]) * gp_sum[0:1, lanes] if shifted else None
         gw = dot(patch_t[k], gp16[:, lanes], ((1,), (0,)))
         gw_out = dot(low_gt, hid[k, :, lanes], ((1,), (0,)))
         for n in range(many):
             at, part = (c + n) * stride, slice(n * LANES, (n + 1) * LANES)
             for o in range(9):
-                flat[at + o * levels:at + (o + 1) * levels] += gw[o * levels:(o + 1) * levels, part] + back[:, part]
+                grown = gw[o * levels:(o + 1) * levels, part]
+                flat[at + o * levels:at + (o + 1) * levels] += grown + back[:, part] if shifted else grown
             flat[at + in_width:at + stride] += gw_out[:, part]
 
     def gradient_low(level_grad):
@@ -485,7 +494,7 @@
     bias_start(0)
     started = 0
     for c in range(0, chunks, 2):
-        weigh(0, low_gt, c, 2)
+        weigh(0, low_gt, c, 2, shifted=False)
         while started < len(groups) and (c + 2 == chunks or groups[started][0] + groups[started][1] <= (c + 2) * stride):
             reduce_start(started, 0)
             started += 1
@@ -610,7 +619,9 @@
             pltpu.VMEM((STEPS, cols, hidden), F32),
             pltpu.VMEM((cols, in_width), BF16),
             pltpu.VMEM((STEPS, in_width, cols), BF16),
-            pltpu.VMEM((2 * width + 2 * rim_rows, in_width), BF16),
+            pltpu.VMEM((2 * width, 3 * levels), BF16),
+            pltpu.VMEM((2, rim_rows, 3 * levels), BF16),
+            pltpu.VMEM((2, 3 * levels, hidden), BF16),
             pltpu.VMEM((cols, hidden), F32),
             pltpu.VMEM((8, hidden), F32),
             pltpu.VMEM((cols, hidden), BF16),

time: 73.7 us -> 73.4 us (level)
  no operation moved by 1% of the time
where the time goes in v2:
time: 73.4 us; the launch traced here: 73.3 us
  Pallas kernels  72.6 us (99%)
    pallas_call x1, Pallas kernels, shards(): pl.pallas_call(functools.partial(chain_kernel, tiles, subs, rows, width,...  71 us
    pallas_call x1, Pallas kernels, shards(): pl.pallas_call(functools.partial(finish_kernel, hidden), out_shape=(jax.S...  1.63 us

profile of v2, /device:TPU:0, one launch (start us, length us, event | category | flops | bytes accessed | tf_op | source)
XLA Modules:
  0.0 73.3 jit_solution(15693339966936321206)
XLA Ops:
  0.6 71.0 %chain.1 = (f32[1,64,256]{2,1,0:T(8,128)S(1)}, f32[1,64,256]{2,1,0:T(8,128)S(1)}, bf16[5120,128]{1,0:T(8,128)(2,1)S(1)}, f32[8,128]{1,0:T(8,128)S(1)}) custom-call(f32[1,64,256]{2,1,0:T(8,128)} %state_hbm.1, f32[1,64,256]{2,1,0:T(8,128)} %cot_hbm.1, bf16[576,1024]{1,0:T(8,128)(2,1)} %w_in_hbm.1, f32[1,1024]{1,0:T(1,128)} %bitcast.2, ...), custom_call_target="tpu_custom_call" | custom-call | tf_op jit(solution)/shard_map/chain/pallas_call | solution.py:573
  71.7 1.6 %finish.1 = (f32[1,64,256]{2,1,0:T(8,128)}, f32[1,64,256]{2,1,0:T(8,128)}, f32[576,1024]{1,0:T(8,128)}, f32[8,128]{1,0:T(8,128)}, f32[64,1024]{1,0:T(8,128)}) custom-call(f32[1,64,256]{2,1,0:T(8,128)S(1)} %get-tuple-element.14.final_in, f32[1,64,256]{2,1,0:T(8,128)S(1)} %get-tuple-element.15.grad_in, bf16[5120,128]{1,0:T(8,128)(2,1)S(1)} %get-tuple-element.16.whole, ...), custom_call_target="tpu_custom_call" | custom-call | tf_op jit(solution)/shard_map/finish/pallas_call | solution.py:637

commit v3 on v2

--- a/solution.py
+++ b/solution.py
@@ -445,7 +445,7 @@
 
     def reduce_start(g, i):
         base, piece, at, bits = stages[g][0][i]
-        for m, copy in enumerate(reduce_copies(g, i), 1):
+        for m, copy in reversed(list(enumerate(reduce_copies(g, i), 1))):
             away = flat[rows_at(base + place_of(bits, m) * piece, piece)]
             out_half[at + (m - 1) * piece:at + m * piece] = away.astype(BF16)
             copy.start()
@@ -508,7 +508,7 @@
                 _, base, size = stages[g]
                 own = rows_at(base, size)
                 whole[own] = flat[own].astype(BF16)
-                for copy in gather_copies(g, depth - 1):
+                for copy in reversed(gather_copies(g, depth - 1)):
                     copy.start()
         if i == 1:
             spread(2 * STEPS - 1, None)
@@ -526,7 +526,7 @@
             for copy in gather_copies(g, i):
                 copy.wait()
             if i > 0:
-                for copy in gather_copies(g, i - 1):
+                for copy in reversed(gather_copies(g, i - 1)):
                     copy.start()
 
 

time: 73.4 us -> 73 us (level)
  no operation moved by 1% of the time
where the time goes in v3:
time: 73 us; the launch traced here: 72.8 us
  Pallas kernels  72.2 us (99%)
    pallas_call x1, Pallas kernels, shards(): pl.pallas_call(functools.partial(chain_kernel, tiles, subs, rows, width,...  70.5 us
    pallas_call x1, Pallas kernels, shards(): pl.pallas_call(functools.partial(finish_kernel, hidden), out_shape=(jax.S...  1.63 us

profile of v3, /device:TPU:0, one launch (start us, length us, event | category | flops | bytes accessed | tf_op | source)
XLA Modules:
  0.0 72.8 jit_solution(17755153939481017703)
XLA Ops:
  0.6 70.5 %chain.1 = (f32[1,64,256]{2,1,0:T(8,128)S(1)}, f32[1,64,256]{2,1,0:T(8,128)S(1)}, bf16[5120,128]{1,0:T(8,128)(2,1)S(1)}, f32[8,128]{1,0:T(8,128)S(1)}) custom-call(f32[1,64,256]{2,1,0:T(8,128)} %state_hbm.1, f32[1,64,256]{2,1,0:T(8,128)} %cot_hbm.1, bf16[576,1024]{1,0:T(8,128)(2,1)} %w_in_hbm.1, f32[1,1024]{1,0:T(1,128)} %bitcast.2, ...), custom_call_target="tpu_custom_call" | custom-call | tf_op jit(solution)/shard_map/chain/pallas_call | solution.py:573
  71.2 1.6 %finish.1 = (f32[1,64,256]{2,1,0:T(8,128)}, f32[1,64,256]{2,1,0:T(8,128)}, f32[576,1024]{1,0:T(8,128)}, f32[8,128]{1,0:T(8,128)}, f32[64,1024]{1,0:T(8,128)}) custom-call(f32[1,64,256]{2,1,0:T(8,128)S(1)} %get-tuple-element.14.final_in, f32[1,64,256]{2,1,0:T(8,128)S(1)} %get-tuple-element.15.grad_in, bf16[5120,128]{1,0:T(8,128)(2,1)S(1)} %get-tuple-element.16.whole, ...), custom_call_target="tpu_custom_call" | custom-call | tf_op jit(solution)/shard_map/finish/pallas_call | solution.py:637
